TPU v7x, 32 devices: a whole 2x2x4 slice. The times are simulated.
32 devices in a mesh: rows: 4 (over x, core), batch: 8 (over z, y).
Axes of the slice: x: 2, y: 2, z: 4, core: 2. Of those that a mesh axis runs over, the one named last changes fastest.
Arguments:
- features: bfloat16 [96, 8, 32, 512], P('batch', 'rows'), may hold values from -12 to 12
- norm_gain: float32 [512], replicated, may hold values from 0.25 to 1.75
- norm_bias: float32 [512], replicated, may hold values from -2.5 to 2.5
- conv_weight: bfloat16 [4, 4608], replicated, may hold values from -0.09375 to 0.09375
- embed_weight: float32 [16, 1024], replicated, may hold values from -1.5 to 1.5
- embed_bias: float32 [1024], replicated, may hold values from -2.5 to 2.5
- proj_in: bfloat16 [1024, 2048], P('rows'), may hold values from -0.1875 to 0.1875
- proj_in_bias: float32 [2048], replicated, may hold values from -2.5 to 2.5
- proj_out: bfloat16 [2048, 768], P('rows'), may hold values from -0.125 to 0.125
- proj_out_bias: float32 [768], replicated, may hold values from -2.5 to 2.5
- targets: bfloat16 [96, 4, 16, 768], P('batch', 'rows'), may hold values from -6 to 6
Outputs:
- grad_features: bfloat16 [96, 8, 32, 512], P('batch', 'rows')
- grad_conv: float32 [4, 4608], replicated
- grad_gain: float32 [512], replicated
- grad_bias: float32 [512], replicated
- grad_embed: float32 [16, 1024], replicated
All inputs are finite; a program needn't handle non-finite values.
Results may differ from a plain program's by a relative error of at most 0.012.
Values may be sent and summed in bfloat16 or wider, within the bound.
A program may use at most 128 MiB of HBM per device.

v0:
```python
import jax
import jax.numpy as jnp
from jax import lax
from jax.sharding import PartitionSpec as P

GROUPS = 32
LATENT = 4
PATCH = 2
ALIGN = 768
EPS_NORM = 1e-06
EPS_UNIT = 1e-06


def padded(block, sides, width):
    for axis, dim in sides:
        count = lax.axis_size(axis)
        forward = [(i, i + 1) for i in range(count - 1)]
        backward = [(target, source) for source, target in forward]
        low = lax.ppermute(
            lax.slice_in_dim(block, block.shape[dim] - width, None, axis=dim), axis, forward
        )
        high = lax.ppermute(lax.slice_in_dim(block, 0, width, axis=dim), axis, backward)
        block = jnp.concatenate([low, block, high], axis=dim)
    return block


def swish_slope(values):
    sig = jax.nn.sigmoid(values)
    return sig * (1.0 + values * (1.0 - sig))


def shards(
    features,
    norm_gain,
    norm_bias,
    conv_weight,
    embed_weight,
    embed_bias,
    proj_in,
    proj_in_bias,
    proj_out,
    proj_out_bias,
    targets,
):
    images, height, across, channels = features.shape
    per_group = channels // GROUPS
    members = lax.axis_size("rows") * height * across * per_group
    cell_count = images * height * across
    values = features.astype(jnp.float32)
    grouped = values.reshape(images, height * across, GROUPS, per_group)
    totals = lax.psum(jnp.sum(grouped, axis=(1, 3)), "rows")
    centred = grouped - (totals / members)[:, None, :, None]
    squares = lax.psum(jnp.sum(centred * centred, axis=(1, 3)), "rows")
    variance = squares / members
    inverse = lax.rsqrt(variance + EPS_NORM)[:, None, :, None]
    normed = (centred * inverse).reshape(images, height, across, channels)
    shifted = normed * norm_gain + norm_bias
    active = (shifted * jax.nn.sigmoid(shifted)).astype(jnp.bfloat16)
    active_flat = active.reshape(cell_count, channels)
    kernel_stack = (
        conv_weight.reshape(LATENT, 9, channels).transpose(2, 1, 0).reshape(channels, 9 * LATENT)
    )
    tap_terms = jnp.dot(active_flat, kernel_stack, preferred_element_type=jnp.float32)
    tap_terms = tap_terms.reshape(images, height, across, 9, LATENT)
    tap_pad = jnp.pad(tap_terms, ((0, 0), (2, 2), (1, 1), (0, 0), (0, 0)))
    extended = jnp.zeros((images, height + 2, across, LATENT), jnp.float32)
    for position in range(9):
        row_off, col_off = (position // 3, position % 3)
        extended = (
            extended
            + tap_pad[:, row_off : row_off + height + 2, col_off : col_off + across, position, :]
        )
    edges = jnp.concatenate([extended[:, 0:1], extended[:, height + 1 : height + 2]], axis=1)
    arrived = padded(edges, (("rows", 1),), 1)
    latent = extended[:, 1 : height + 1]
    latent = latent.at[:, 0].add(arrived[:, 0])
    latent = latent.at[:, height - 1].add(arrived[:, 3])
    tok_rows = height // PATCH
    tok_cols = across // PATCH
    tok_count = images * tok_rows * tok_cols
    patches = (
        latent.reshape(images, tok_rows, PATCH, tok_cols, PATCH, LATENT)
        .transpose(0, 1, 3, 2, 4, 5)
        .reshape(tok_count, PATCH * PATCH * LATENT)
    )
    embedded = (
        jnp.dot(patches, embed_weight, precision=lax.Precision.HIGHEST) + embed_bias
    ).astype(jnp.bfloat16)
    full_in, full_out = (
        lax.all_gather(proj_in, "rows", axis=0, tiled=True),
        lax.all_gather(proj_out, "rows", axis=0, tiled=True),
    )
    hidden_pre = jnp.dot(embedded, full_in, preferred_element_type=jnp.float32) + proj_in_bias
    hidden_act = (hidden_pre * jax.nn.sigmoid(hidden_pre)).astype(jnp.bfloat16)
    projected = jnp.dot(hidden_act, full_out, preferred_element_type=jnp.float32) + proj_out_bias
    target = targets.reshape(tok_count, ALIGN).astype(jnp.float32)
    unit_target = target * lax.rsqrt(jnp.sum(target * target, axis=1, keepdims=True) + EPS_UNIT)
    inv_len = lax.rsqrt(jnp.sum(projected * projected, axis=1, keepdims=True) + EPS_UNIT)
    unit_proj = projected * inv_len
    cosine = jnp.sum(unit_proj * unit_target, axis=1, keepdims=True)
    grad_out = (-inv_len * (unit_target - cosine * unit_proj)).astype(jnp.bfloat16)
    back_hidden = lax.dot_general(
        grad_out, full_out, (((1,), (1,)), ((), ())), preferred_element_type=jnp.float32
    )
    grad_hidden = (back_hidden * swish_slope(hidden_pre)).astype(jnp.bfloat16)
    grad_embedded = lax.dot_general(
        grad_hidden, full_in, (((1,), (1,)), ((), ())), preferred_element_type=jnp.float32
    )
    embed_part = lax.dot_general(
        patches, grad_embedded, (((0,), (0,)), ((), ())), precision=lax.Precision.HIGHEST
    )
    grad_patch = lax.dot_general(
        grad_embedded, embed_weight, (((1,), (1,)), ((), ())), precision=lax.Precision.HIGHEST
    )
    grad_latent = (
        grad_patch.reshape(images, tok_rows, tok_cols, PATCH, PATCH, LATENT)
        .transpose(0, 1, 3, 2, 4, 5)
        .reshape(images, height, across, LATENT)
        .astype(jnp.bfloat16)
    )
    grad_pad = padded(grad_latent, (("rows", 1),), 1)
    grad_pad = jnp.pad(grad_pad, ((0, 0), (0, 0), (1, 1), (0, 0)))
    shifted_grads = []
    for position in range(9):
        row_off, col_off = (position // 3, position % 3)
        shifted_grads.append(
            grad_pad[:, 2 - row_off : 2 - row_off + height, 2 - col_off : 2 - col_off + across, :]
        )
    grad_taps = jnp.concatenate(shifted_grads, axis=3).reshape(cell_count, 9 * LATENT)
    conv_stack = lax.dot_general(
        active_flat, grad_taps, (((0,), (0,)), ((), ())), preferred_element_type=jnp.float32
    )
    conv_part = (
        conv_stack.reshape(channels, 9, LATENT).transpose(2, 1, 0).reshape(LATENT, 9 * channels)
    )
    grad_active = lax.dot_general(
        grad_taps, kernel_stack, (((1,), (1,)), ((), ())), preferred_element_type=jnp.float32
    )
    flat_shift = shifted.reshape(cell_count, channels)
    flat_normed = normed.reshape(cell_count, channels)
    grad_shift = grad_active * swish_slope(flat_shift)
    gain_part = jnp.sum(grad_shift * flat_normed, axis=0)
    bias_part = jnp.sum(grad_shift, axis=0)
    grad_norm = (grad_shift * norm_gain).reshape(images, height * across, GROUPS, per_group)
    normed_groups = flat_normed.reshape(images, height * across, GROUPS, per_group)
    first, second = lax.psum(
        (jnp.sum(grad_norm, axis=(1, 3)), jnp.sum(grad_norm * normed_groups, axis=(1, 3))), "rows"
    )
    grad_values = inverse * (
        grad_norm
        - (first / members)[:, None, :, None]
        - normed_groups * (second / members)[:, None, :, None]
    )
    grad_features = grad_values.reshape(images, height, across, channels).astype(jnp.bfloat16)
    grad_conv, grad_gain, grad_bias, grad_embed = lax.psum(
        (conv_part, gain_part, bias_part, embed_part), ("rows", "batch")
    )
    return (grad_features, grad_conv, grad_gain, grad_bias, grad_embed)


def solution(mesh):
    in_specs = (
        P("batch", "rows", None, None),
        P(),
        P(),
        P(),
        P(),
        P(),
        P("rows", None),
        P(),
        P("rows", None),
        P(),
        P("batch", "rows", None, None),
    )
    out_specs = (P("batch", "rows", None, None), P(), P(), P(), P())
    return jax.shard_map(shards, mesh=mesh, in_specs=in_specs, out_specs=out_specs, check_vma=False)
```

profile of v0, /device:TPU:8, one launch (start us, length us, event | category | flops | bytes accessed | tf_op | source)
XLA Modules:
  0.0 264.1 jit_solution(803283353714649149)
XLA Ops:
  9.3 7.0 %psum.56 = f32[12,32]{1,0:T(8,128)S(1)} all-reduce(f32[12,32]{1,0:T(8,128)S(1)} %reduce_sum.97), channel_id=1, replica_groups=mesh['rows'=4,'batch'=8] {'rows'}, use_global_device_ids=true, to_apply=%region_2.0 | all-reduce | flops 384 | bytes 3072 | tf_op jit(solution)/shard_map/psum | solution.py:51
  17.1 6.2 %psum.57 = f32[12,32]{1,0:T(8,128)S(1)} all-reduce(f32[12,32]{1,0:T(8,128)S(1)} %reduce_sum.100), channel_id=1, replica_groups=mesh['rows'=4,'batch'=8] {'rows'}, use_global_device_ids=true, to_apply=%region_5.6 | all-reduce | flops 384 | bytes 3072 | tf_op jit(solution)/shard_map/psum | solution.py:53
  23.6 1.7 multiply_convert_fusion.2
  28.7 3.6 %collective-permute-start = (f32[12,1,32,4]{2,3,1,0:T(4,128)}, f32[12,1,32,4]{2,3,1,0:T(4,128)}, u32[]{:S(2)}, u32[]{:S(2)}) collective-permute-start(f32[12,1,32,4]{2,3,1,0:T(4,128)} %get-tuple-element.43), channel_id=1, source_target_pairs={{0,8},{8,16},{16,24},{1,9},{9,17},{17,25},{2,10},{10,18},{18,26},{... | collective-permute-start | bytes 18440 | tf_op jit(solution)/shard_map/ppermute | solution.py:19
  33.7 6.2 %copy.155 = f32[12,2,32,512]{2,1,0,3:T(2,128)} copy(bf16[12,2,32,512]{3,2,1,0:T(8,128)(2,1)S(1)} %copy-done.1) | data formatting | bytes 2359296 | tf_op jit(solution)/shard_map/reshape | solution.py:50
  39.9 2.4 mul.163
  42.3 3.4 %mul.171 = f32[768,512]{0,1:T(8,128)S(1)} reshape(f32[12,64,32,16]{1,0,3,2:T(8,128)} %mul.163) | data formatting | bytes 3145728 | tf_op jit(solution)/shard_map/mul | solution.py:149
  45.7 1.6 copy.150
  47.3 2.4 sub.61
  49.7 3.3 %sub.64 = f32[768,512]{0,1:T(8,128)S(1)} reshape(f32[12,64,32,16]{1,0,3,2:T(8,128)} %sub.61) | data formatting | bytes 3145728 | tf_op jit(solution)/shard_map/sub | solution.py:52
  53.1 1.6 copy.149
  54.7 7.8 %reshape.201 = f32[12,64,32,16]{1,0,3,2:T(8,128)} reshape(f32[12,2,32,512]{2,1,0,3:T(2,128)} %copy.155) | data formatting | bytes 3145728 | tf_op jit(solution)/shard_map/reshape | solution.py:50
  64.6 4.3 %convolution_add_fusion = f32[192,2048]{1,0:T(8,128)} fusion(bf16[192,1024]{1,0:T(8,128)(2,1)S(1)} %fusion.10, bf16[1024,2048]{1,0:T(8,128)(2,1)} %all-gather.3.cloned.1.call-done, f32[2048]{0:T(1024)S(1)} %copy-done.6), kind=kOutput, calls=%fused_computation.11 | convolution fusion | flops 805699584 | bytes 6168576 | tf_op jit(solution)/shard_map/dot_general | solution.py:93
  68.9 6.9 %all-gather.5.cloned.1.call-done = bf16[2048,768]{1,0:T(8,128)(2,1)} async-done(((bf16[512,768]{1,0:T(8,128)(2,1)}), bf16[2048,768]{1,0:T(8,128)(2,1)}) %all-gather.5.cloned.1.call-update) | async-done | bytes 3145744 | tf_op jit(solution)/shard_map/all_gather | solution.py:91
  75.8 3.4 %multiply_reduce_fusion.4 = (f32[192]{0:T(256)S(1)}, f32[192,768]{1,0:T(8,128)S(1)}) fusion(f32[768]{0:T(1024)S(1)} %copy-done.10, bf16[2048,768]{1,0:T(8,128)(2,1)} %all-gather.5.cloned.1.call-done, f32[192,2048]{1,0:T(8,128)} %convolution_add_fusion), kind=kOutput, calls=%fused_computation.47 | convolution fusion | flops 606388032 | bytes 5312256 | tf_op jit(solution)/shard_map/dot_general | solution.py:95
  80.1 6.4 %fusion.11 = f32[192,1024]{1,0:T(8,128)S(1)} fusion(bf16[1024,2048]{1,0:T(8,128)(2,1)} %all-gather.3.cloned.1.call-done, bf16[2048,768]{1,0:T(8,128)(2,1)} %all-gather.5.cloned.1.call-done, f32[192,2048]{1,0:T(8,128)} %convolution_add_fusion, f32[192,768]{1,0:T(8,128)S(1)} %copy-done.2, f32[192,768]{1,0:T(8,128)} %copy-done.4, ...), kind=kOutput, calls=%fused_computation.37 | convolution fusion | flops 1413562368 | bytes 10881280 | tf_op jit(solution)/shard_map/dot_general | solution.py:106
  87.5 2.1 collective-permute-start.2
  101.4 3.3 %fusion.46 = (f32[512]{0:T(512)S(1)}, f32[512]{0:T(512)S(1)}, f32[768,512]{1,0:T(8,128)S(1)}) fusion(f32[768,512]{1,0:T(8,128)} %copy.150, f32[768,512]{1,0:T(8,128)} %copy.149, bf16[12,2,32,512]{3,2,1,0:T(8,128)(2,1)S(1)} %copy-done.1, f32[512]{0:T(512)S(1)} %copy-done.9, f32[12,2,32,512]{3,2,1,0:T(8,128)} %get-tuple-element.41, ...), kind=kOutput, calls=%fused_computation.94 | convolution fusion | flops 34208768 | bytes 7176192 | tf_op jit(solution)/shard_map/dot_general | solution.py:136
  104.7 1.6 copy.141
  106.3 4.0 %reshape.188 = f32[12,64,32,16]{1,0,3,2:T(8,128)} reshape(f32[768,512]{0,1:T(8,128)} %copy.141) | data formatting | bytes 3145728 | tf_op jit(solution)/shard_map/reshape | solution.py:144
  110.3 4.7 %fusion.45 = (f32[12,32]{0,1:T(8,128)S(1)}, f32[12,32]{0,1:T(8,128)S(1)}) fusion(f32[12,64,32,16]{1,0,3,2:T(8,128)} %reshape.188, f32[12,32]{0,1:T(8,128)S(1)} %copy.146, f32[12,64,32,16]{1,0,3,2:T(8,128)} %reshape.201, f32[12,32]{0,1:T(8,128)S(1)} %copy.144), kind=kLoop, calls=%fused_computation.93 | loop fusion | flops 1965312 | bytes 3151872 | tf_op jit(solution)/shard_map/reduce_sum | solution.py:147
  115.2 12.6 %all-reduce.4 = (f32[12,32]{1,0:T(8,128)S(1)}, f32[12,32]{1,0:T(8,128)S(1)}) all-reduce(f32[12,32]{1,0:T(8,128)S(1)} %copy.147, f32[12,32]{1,0:T(8,128)S(1)} %copy.142), channel_id=1, replica_groups=mesh['rows'=4,'batch'=8] {'rows'}, use_global_device_ids=true, to_apply=%region_12.13 | all-reduce | flops 768 | bytes 6144 | tf_op jit(solution)/shard_map/psum | solution.py:146
  129.6 40.3 %all-reduce.2 = (f32[512]{0:T(512)}, f32[512]{0:T(512)}) all-reduce(f32[512]{0:T(512)S(1)} %get-tuple-element.32, f32[512]{0:T(512)S(1)} %get-tuple-element.31), channel_id=1, replica_groups=mesh['rows'=4,'batch'=8] {'rows','batch'}, use_global_device_ids=true, to_apply=%region_15.16 | all-reduce | flops 1024 | bytes 8192 | tf_op jit(solution)/shard_map/psum | solution.py:155
  169.9 84.6 %all-reduce.7.cloned.1.call-done = (f32[4,4608]{1,0:T(4,128)}, f32[16,1024]{1,0:T(8,128)}) async-done(((f32[4,4608]{1,0:T(4,128)}, f32[16,1024]{1,0:T(8,128)}), (f32[4,4608]{1,0:T(4,128)}, f32[16,1024]{1,0:T(8,128)})) %all-reduce.7.cloned.1.call-update) | async-done | bytes 139280 | tf_op jit(solution)/shard_map/psum | solution.py:155
  (99 shorter events, 28.1 us)
Async XLA Ops:
  7.2 56.6 %copy-start = (f32[16,1024]{1,0:T(8,128)S(1)}, f32[16,1024]{1,0:T(8,128)}, u32[]{:S(2)}) copy-start(f32[16,1024]{1,0:T(8,128)} %param.19) | copy-start | bytes 196612
  7.2 1.6 copy-start.5
  7.2 1.7 copy-start.1
  7.2 57.4 %all-gather.3.cloned.1.call-start = ((), (), s32[]{:S(2)}) async-start(), calls=%async_computation | async-start | bytes 5242880 | tf_op jit(solution)/shard_map/all_gather | solution.py:90
  7.9 67.9 %all-gather.5.cloned.1.call-start = ((), (), s32[]{:S(2)}) async-start(), calls=%async_computation.1 | async-start | bytes 3932160 | tf_op jit(solution)/shard_map/all_gather | solution.py:91
  8.7 245.9 %all-reduce.7.cloned.1.call-start = ((), (), s32[]{:S(2)}) async-start(), calls=%async_computation.2 | async-start | bytes 278528 | tf_op jit(solution)/shard_map/psum | solution.py:155
  8.9 14.7 %copy-start.8 = (f32[512]{0:T(512)S(1)}, f32[512]{0:T(512)}, u32[]{:S(2)}) copy-start(f32[512]{0:T(512)} %param.17) | copy-start | bytes 6148
  8.9 14.7 %copy-start.9 = (f32[512]{0:T(512)S(1)}, f32[512]{0:T(512)}, u32[]{:S(2)}) copy-start(f32[512]{0:T(512)} %param.16) | copy-start | bytes 6148
  25.3 7.0 %copy-start.3 = (bf16[12,1,16,768]{3,2,1,0:T(8,128)(2,1)S(1)}, bf16[12,1,16,768]{3,2,1,0:T(8,128)(2,1)}, u32[]{:S(2)}) copy-start(bf16[12,1,16,768]{3,2,1,0:T(8,128)(2,1)} %param.25) | copy-start | bytes 884740
  27.4 35.9 %collective-permute-start.1 = (f32[12,1,32,4]{2,3,1,0:T(4,128)S(1)}, f32[12,1,32,4]{2,3,1,0:T(4,128)S(1)}, u32[]{:S(2)}, u32[]{:S(2)}) collective-permute-start(f32[12,1,32,4]{2,3,1,0:T(4,128)S(1)} %get-tuple-element.42), channel_id=1, source_target_pairs={{8,0},{16,8},{24,16},{9,1},{17,9},{25,17},{10,2},{18,10},{26,18},{... | collective-permute-start | bytes 18440 | tf_op jit(solution)/shard_map/ppermute | solution.py:22
  28.7 33.8 %collective-permute-start = (f32[12,1,32,4]{2,3,1,0:T(4,128)}, f32[12,1,32,4]{2,3,1,0:T(4,128)}, u32[]{:S(2)}, u32[]{:S(2)}) collective-permute-start(f32[12,1,32,4]{2,3,1,0:T(4,128)} %get-tuple-element.43), channel_id=1, source_target_pairs={{0,8},{8,16},{16,24},{1,9},{9,17},{17,25},{2,10},{10,18},{18,26},{... | collective-permute-start | bytes 18440 | tf_op jit(solution)/shard_map/ppermute | solution.py:19
  54.7 9.0 %copy-start.7 = (f32[1024]{0:T(1024)S(1)}, f32[1024]{0:T(1024)}, u32[]{:S(2)}) copy-start(f32[1024]{0:T(1024)} %param.20) | copy-start | bytes 12292
  54.7 9.9 %copy-start.6 = (f32[2048]{0:T(1024)S(1)}, f32[2048]{0:T(1024)}, u32[]{:S(2)}) copy-start(f32[2048]{0:T(1024)} %param.22) | copy-start | bytes 24580
  64.6 11.3 %copy-start.10 = (f32[768]{0:T(1024)S(1)}, f32[768]{0:T(1024)}, u32[]{:S(2)}) copy-start(f32[768]{0:T(1024)} %param.24) | copy-start | bytes 9220
  68.9 10.3 %copy-start.2 = (f32[192,768]{1,0:T(8,128)S(1)}, f32[192,768]{1,0:T(8,128)}, u32[]{:S(2)}) copy-start(f32[192,768]{1,0:T(8,128)} %bitcast_multiply_fusion.1) | copy-start | bytes 1769476
  79.3 0.8 copy-start.4
  87.5 4.8 %collective-permute-start.2 = (bf16[12,1,32,4]{0,2,3,1:T(8,128)(2,1)S(1)}, bf16[12,1,32,4]{0,2,3,1:T(8,128)(2,1)S(1)}, u32[]{:S(2)}, u32[]{:S(2)}) collective-permute-start(bf16[12,1,32,4]{0,2,3,1:T(8,128)(2,1)S(1)} %get-tuple-element.44), channel_id=1, source_target_pairs={{0,8},{8,16},{16,24},{1,9},{9,17},{17,25},{2,10},{10,18},{18,26},{... | collective-permute-start | bytes 9224 | tf_op jit(solution)/shard_map/ppermute | solution.py:19
  89.7 3.1 %collective-permute-start.3 = (bf16[12,1,32,4]{0,2,3,1:T(8,128)(2,1)S(1)}, bf16[12,1,32,4]{0,2,3,1:T(8,128)(2,1)S(1)}, u32[]{:S(2)}, u32[]{:S(2)}) collective-permute-start(bf16[12,1,32,4]{0,2,3,1:T(8,128)(2,1)S(1)} %get-tuple-element.45), channel_id=1, source_target_pairs={{8,0},{16,8},{24,16},{9,1},{17,9},{25,17},{10,2},{18,10},{26,18},{... | collective-permute-start | bytes 9224 | tf_op jit(solution)/shard_map/ppermute | solution.py:22
Sparse Core Ops, SparseCore 0:
  9.6 36.0 all-gather.2
  47.2 28.5 all-gather.4
  128.4 126.0 all-reduce.6
where the time goes:
time: 265 us; the launch traced here: 264 us
  waiting for transfers between devices  93.4 us (35%)
  blocking collectives  66.2 us (25%)
  local copies, waits for them, and re-layouts  48 us (18%)
  matrix products  21.2 us (8%)
  between operations  14.2 us (5%)
  other arithmetic  12.5 us (5%)
  starting transfers between devices  8.67 us (3%)
    psum x1, waiting for transfers between devices, shards(): lax.psum((conv_part, gain_part, bias_part, embed_part), ('rows', 'batch'))  84.6 us
    psum x1, blocking collectives, shards(): lax.psum((conv_part, gain_part, bias_part, embed_part), ('rows', 'batch'))  40.3 us
    reshape x2, local copies, waits for them, and re-layouts, shards(): grouped = values.reshape(images, height * across, GROUPS, per_group)  14 us
    psum x1, blocking collectives, shards(): lax.psum((jnp.sum(grad_norm, axis=(1, 3)), jnp.sum(grad_norm * normed_gro...  12.6 us
    unnamed x31, local copies, waits for them, and re-layouts  8.16 us
    sub x5, local copies, waits for them, and re-layouts, shards(): centred = grouped - (totals / members)[:, None, :, None]  7.65 us
    mul x5, local copies, waits for them, and re-layouts, shards(): inverse * (grad_norm - (first / members)[:, None, :, None] - normed_group...  7.62 us
    psum x1, blocking collectives, shards(): totals = lax.psum(jnp.sum(grouped, axis=(1, 3)), 'rows')  7.05 us
  transfers between devices with their start and end apart: 7, of which 3 were waited for; matrix products, arithmetic and copies ran while one was open for 17% of the time, Pallas kernels for 0%

commit v1 on v0

--- a/solution.py
+++ b/solution.py
@@ -153,7 +153,7 @@
     )
     grad_features = grad_values.reshape(images, height, across, channels).astype(jnp.bfloat16)
     grad_conv, grad_gain, grad_bias, grad_embed = lax.psum(
-        (conv_part, gain_part, bias_part, embed_part), ("rows", "batch")
+        lax.psum((conv_part, gain_part, bias_part, embed_part), "batch"), "rows"
     )
     return (grad_features, grad_conv, grad_gain, grad_bias, grad_embed)
 

time: 265 us -> 232 us (0.88)
  blocking collectives: 66.2 us -> 43.3 us
  waiting for transfers between devices: 93.4 us -> 81.8 us
    psum x1, blocking collectives: 40.3 us -> 18.6 us  [shards(): lax.psum((conv_part, gain_part, bias_part, embed_part), 'batch')]
    psum x1 -> x2, waiting for transfers between devices: 84.6 us -> 73 us  [the longest x1 41.8 us: shards(): lax.psum((conv_part, gain_part, bias_part, embed_part), 'batch')]
  transfers between devices with their start and end apart: 7 -> 8, of which waited for: 3 -> 4; matrix products, arithmetic and copies ran while one was open for 17% -> 19% of each run, Pallas kernels for 0% -> 0%
where the time goes in v1:
time: 232 us; the launch traced here: 230 us
  waiting for transfers between devices  81.8 us (35%)
  local copies, waits for them, and re-layouts  48 us (21%)
  blocking collectives  43.3 us (19%)
  matrix products  21.2 us (9%)
  between operations  14.2 us (6%)
  other arithmetic  12.5 us (5%)
  starting transfers between devices  8.72 us (4%)
    psum x1, waiting for transfers between devices, shards(): lax.psum((conv_part, gain_part, bias_part, embed_part), 'batch')  41.8 us
    psum x1, waiting for transfers between devices, shards(): lax.psum(lax.psum((conv_part, gain_part, bias_part, embed_part), 'batch')...  31.1 us
    psum x1, blocking collectives, shards(): lax.psum((conv_part, gain_part, bias_part, embed_part), 'batch')  18.6 us
    reshape x2, local copies, waits for them, and re-layouts, shards(): grouped = values.reshape(images, height * across, GROUPS, per_group)  14 us
    psum x1, blocking collectives, shards(): lax.psum((jnp.sum(grad_norm, axis=(1, 3)), jnp.sum(grad_norm * normed_gro...  11.4 us
    unnamed x31, local copies, waits for them, and re-layouts  8.16 us
    sub x5, local copies, waits for them, and re-layouts, shards(): centred = grouped - (totals / members)[:, None, :, None]  7.65 us
    mul x5, local copies, waits for them, and re-layouts, shards(): inverse * (grad_norm - (first / members)[:, None, :, None] - normed_group...  7.62 us
  transfers between devices with their start and end apart: 8, of which 4 were waited for; matrix products, arithmetic and copies ran while one was open for 19% of the time, Pallas kernels for 0%

profile of v1, /device:TPU:8, one launch (start us, length us, event | category | flops | bytes accessed | tf_op | source)
XLA Modules:
  0.0 229.6 jit_solution(9858763514412575561)
XLA Ops:
  9.3 7.0 %psum.84 = f32[12,32]{1,0:T(8,128)S(1)} all-reduce(f32[12,32]{1,0:T(8,128)S(1)} %reduce_sum.97), channel_id=1, replica_groups=mesh['rows'=4,'batch'=8] {'rows'}, use_global_device_ids=true, to_apply=%region_2.0 | all-reduce | flops 384 | bytes 3072 | tf_op jit(solution)/shard_map/psum | solution.py:51
  17.1 6.2 %psum.85 = f32[12,32]{1,0:T(8,128)S(1)} all-reduce(f32[12,32]{1,0:T(8,128)S(1)} %reduce_sum.100), channel_id=1, replica_groups=mesh['rows'=4,'batch'=8] {'rows'}, use_global_device_ids=true, to_apply=%region_5.6 | all-reduce | flops 384 | bytes 3072 | tf_op jit(solution)/shard_map/psum | solution.py:53
  23.6 1.7 multiply_convert_fusion.2
  28.7 3.6 %collective-permute-start = (f32[12,1,32,4]{2,3,1,0:T(4,128)}, f32[12,1,32,4]{2,3,1,0:T(4,128)}, u32[]{:S(2)}, u32[]{:S(2)}) collective-permute-start(f32[12,1,32,4]{2,3,1,0:T(4,128)} %get-tuple-element.47), channel_id=1, source_target_pairs={{0,8},{8,16},{16,24},{1,9},{9,17},{17,25},{2,10},{10,18},{18,26},{... | collective-permute-start | bytes 18440 | tf_op jit(solution)/shard_map/ppermute | solution.py:19
  33.7 6.2 %copy.155 = f32[12,2,32,512]{2,1,0,3:T(2,128)} copy(bf16[12,2,32,512]{3,2,1,0:T(8,128)(2,1)S(1)} %copy-done.1) | data formatting | bytes 2359296 | tf_op jit(solution)/shard_map/reshape | solution.py:50
  39.9 2.4 %mul.163 = f32[12,64,32,16]{1,0,3,2:T(8,128)} broadcast(f32[12,32]{0,1:T(8,128)S(1)} %copy.146), dimensions={0,2} | broadcast | bytes 1574400 | tf_op jit(solution)/shard_map/mul | solution.py:149
  42.3 3.4 %mul.171 = f32[768,512]{0,1:T(8,128)S(1)} reshape(f32[12,64,32,16]{1,0,3,2:T(8,128)} %mul.163) | data formatting | bytes 3145728 | tf_op jit(solution)/shard_map/mul | solution.py:149
  47.3 2.4 %sub.61 = f32[12,64,32,16]{1,0,3,2:T(8,128)} broadcast(f32[12,32]{0,1:T(8,128)S(1)} %copy.144), dimensions={0,2} | broadcast | bytes 1574400 | tf_op jit(solution)/shard_map/sub | solution.py:52
  49.7 3.3 %sub.64 = f32[768,512]{0,1:T(8,128)S(1)} reshape(f32[12,64,32,16]{1,0,3,2:T(8,128)} %sub.61) | data formatting | bytes 3145728 | tf_op jit(solution)/shard_map/sub | solution.py:52
  53.1 1.6 copy.149
  54.7 7.8 %reshape.201 = f32[12,64,32,16]{1,0,3,2:T(8,128)} reshape(f32[12,2,32,512]{2,1,0,3:T(2,128)} %copy.155) | data formatting | bytes 3145728 | tf_op jit(solution)/shard_map/reshape | solution.py:50
  64.6 4.3 %convolution_add_fusion = f32[192,2048]{1,0:T(8,128)} fusion(bf16[192,1024]{1,0:T(8,128)(2,1)S(1)} %fusion.10, bf16[1024,2048]{1,0:T(8,128)(2,1)} %all-gather.3.cloned.1.call-done, f32[2048]{0:T(1024)S(1)} %copy-done.6), kind=kOutput, calls=%fused_computation.11 | convolution fusion | flops 805699584 | bytes 6168576 | tf_op jit(solution)/shard_map/dot_general | solution.py:93
  68.9 6.9 %all-gather.5.cloned.1.call-done = bf16[2048,768]{1,0:T(8,128)(2,1)} async-done(((bf16[512,768]{1,0:T(8,128)(2,1)}), bf16[2048,768]{1,0:T(8,128)(2,1)}) %all-gather.5.cloned.1.call-update) | async-done | bytes 3145744 | tf_op jit(solution)/shard_map/all_gather | solution.py:91
  75.8 3.4 %multiply_reduce_fusion.4 = (f32[192]{0:T(256)S(1)}, f32[192,768]{1,0:T(8,128)S(1)}) fusion(f32[768]{0:T(1024)S(1)} %copy-done.10, bf16[2048,768]{1,0:T(8,128)(2,1)} %all-gather.5.cloned.1.call-done, f32[192,2048]{1,0:T(8,128)} %convolution_add_fusion), kind=kOutput, calls=%fused_computation.47 | convolution fusion | flops 606388032 | bytes 5312256 | tf_op jit(solution)/shard_map/dot_general | solution.py:95
  80.1 6.4 %fusion.11 = f32[192,1024]{1,0:T(8,128)S(1)} fusion(bf16[1024,2048]{1,0:T(8,128)(2,1)} %all-gather.3.cloned.1.call-done, bf16[2048,768]{1,0:T(8,128)(2,1)} %all-gather.5.cloned.1.call-done, f32[192,2048]{1,0:T(8,128)} %convolution_add_fusion, f32[192,768]{1,0:T(8,128)S(1)} %copy-done.2, f32[192,768]{1,0:T(8,128)} %copy-done.4, ...), kind=kOutput, calls=%fused_computation.37 | convolution fusion | flops 1413562368 | bytes 10881280 | tf_op jit(solution)/shard_map/dot_general | solution.py:106
  87.5 2.1 collective-permute-start.2
  101.4 3.3 %fusion.46 = (f32[512]{0:T(512)S(1)}, f32[512]{0:T(512)S(1)}, f32[768,512]{1,0:T(8,128)S(1)}) fusion(f32[768,512]{1,0:T(8,128)} %copy.150, f32[768,512]{1,0:T(8,128)} %copy.149, bf16[12,2,32,512]{3,2,1,0:T(8,128)(2,1)S(1)} %copy-done.1, f32[512]{0:T(512)S(1)} %copy-done.9, f32[12,2,32,512]{3,2,1,0:T(8,128)} %get-tuple-element.45, ...), kind=kOutput, calls=%fused_computation.94 | convolution fusion | flops 34208768 | bytes 7176192 | tf_op jit(solution)/shard_map/dot_general | solution.py:136
  104.7 1.6 copy.141
  106.3 4.0 %reshape.188 = f32[12,64,32,16]{1,0,3,2:T(8,128)} reshape(f32[768,512]{0,1:T(8,128)} %copy.141) | data formatting | bytes 3145728 | tf_op jit(solution)/shard_map/reshape | solution.py:144
  110.3 4.7 %fusion.45 = (f32[12,32]{0,1:T(8,128)S(1)}, f32[12,32]{0,1:T(8,128)S(1)}) fusion(f32[12,64,32,16]{1,0,3,2:T(8,128)} %reshape.188, f32[12,32]{0,1:T(8,128)S(1)} %copy.146, f32[12,64,32,16]{1,0,3,2:T(8,128)} %reshape.201, f32[12,32]{0,1:T(8,128)S(1)} %copy.144), kind=kLoop, calls=%fused_computation.93 | loop fusion | flops 1965312 | bytes 3151872 | tf_op jit(solution)/shard_map/reduce_sum | solution.py:147
  115.3 18.6 %all-reduce.2 = (f32[512]{0:T(512)S(1)}, f32[512]{0:T(512)S(1)}) all-reduce(f32[512]{0:T(512)S(1)} %get-tuple-element.32, f32[512]{0:T(512)S(1)} %get-tuple-element.31), channel_id=1, replica_groups=mesh['rows'=4,'batch'=8] {'batch'}, use_global_device_ids=true, to_apply=%region_16.17 | all-reduce | flops 1024 | bytes 8192 | tf_op jit(solution)/shard_map/psum | solution.py:156
  133.9 11.4 %all-reduce.4 = (f32[12,32]{1,0:T(8,128)S(1)}, f32[12,32]{1,0:T(8,128)S(1)}, f32[512]{0:T(512)}, f32[512]{0:T(512)}) all-reduce(f32[12,32]{1,0:T(8,128)S(1)} %copy.147, f32[12,32]{1,0:T(8,128)S(1)} %copy.142, f32[512]{0:T(512)S(1)} %get-tuple-element.33, f32[512]{0:T(512)S(1)} %get-tuple-element.34), channel_id=1, replica_groups=mesh['rows'=4,'batch'=8] {'rows'}, use_global_device_ids=true, to_apply=%region_12.13 | all-reduce | flops 1792 | bytes 14336 | tf_op jit(solution)/shard_map/psum | solution.py:146
  145.8 41.8 %all-reduce.9.cloned.1.call-done = (f32[4,4608]{1,0:T(4,128)}, f32[16,1024]{1,0:T(8,128)}) async-done(((f32[4,4608]{1,0:T(4,128)}, f32[16,1024]{1,0:T(8,128)}), (f32[4,4608]{1,0:T(4,128)}, f32[16,1024]{1,0:T(8,128)})) %all-reduce.9.cloned.1.call-update) | async-done | bytes 139280 | tf_op jit(solution)/shard_map/psum | solution.py:156
  189.0 31.1 %all-reduce.11.cloned.1.call-done = (f32[4,4608]{1,0:T(4,128)}, f32[16,1024]{1,0:T(8,128)}) async-done(((f32[4,4608]{1,0:T(4,128)}, f32[16,1024]{1,0:T(8,128)}), (f32[4,4608]{1,0:T(4,128)}, f32[16,1024]{1,0:T(8,128)})) %all-reduce.11.cloned.1.call-update) | async-done | bytes 139280 | tf_op jit(solution)/shard_map/psum | solution.py:155
  (102 shorter events, 29.8 us)
Async XLA Ops:
  7.2 56.6 %copy-start = (f32[16,1024]{1,0:T(8,128)S(1)}, f32[16,1024]{1,0:T(8,128)}, u32[]{:S(2)}) copy-start(f32[16,1024]{1,0:T(8,128)} %param.19) | copy-start | bytes 196612
  7.2 1.6 copy-start.5
  7.2 1.7 copy-start.1
  7.2 57.4 %all-gather.3.cloned.1.call-start = ((), (), s32[]{:S(2)}) async-start(), calls=%async_computation | async-start | bytes 5242880 | tf_op jit(solution)/shard_map/all_gather | solution.py:90
  7.9 67.9 %all-gather.5.cloned.1.call-start = ((), (), s32[]{:S(2)}) async-start(), calls=%async_computation.1 | async-start | bytes 3932160 | tf_op jit(solution)/shard_map/all_gather | solution.py:91
  8.7 178.9 %all-reduce.9.cloned.1.call-start = ((), (), s32[]{:S(2)}) async-start(), calls=%async_computation.2 | async-start | bytes 278528 | tf_op jit(solution)/shard_map/psum | solution.py:156
  8.9 14.7 %copy-start.8 = (f32[512]{0:T(512)S(1)}, f32[512]{0:T(512)}, u32[]{:S(2)}) copy-start(f32[512]{0:T(512)} %param.17) | copy-start | bytes 6148
  8.9 14.7 %copy-start.9 = (f32[512]{0:T(512)S(1)}, f32[512]{0:T(512)}, u32[]{:S(2)}) copy-start(f32[512]{0:T(512)} %param.16) | copy-start | bytes 6148
  25.3 7.0 %copy-start.3 = (bf16[12,1,16,768]{3,2,1,0:T(8,128)(2,1)S(1)}, bf16[12,1,16,768]{3,2,1,0:T(8,128)(2,1)}, u32[]{:S(2)}) copy-start(bf16[12,1,16,768]{3,2,1,0:T(8,128)(2,1)} %param.25) | copy-start | bytes 884740
  27.4 35.9 %collective-permute-start.1 = (f32[12,1,32,4]{2,3,1,0:T(4,128)S(1)}, f32[12,1,32,4]{2,3,1,0:T(4,128)S(1)}, u32[]{:S(2)}, u32[]{:S(2)}) collective-permute-start(f32[12,1,32,4]{2,3,1,0:T(4,128)S(1)} %get-tuple-element.46), channel_id=1, source_target_pairs={{8,0},{16,8},{24,16},{9,1},{17,9},{25,17},{10,2},{18,10},{26,18},{... | collective-permute-start | bytes 18440 | tf_op jit(solution)/shard_map/ppermute | solution.py:22
  28.7 33.8 %collective-permute-start = (f32[12,1,32,4]{2,3,1,0:T(4,128)}, f32[12,1,32,4]{2,3,1,0:T(4,128)}, u32[]{:S(2)}, u32[]{:S(2)}) collective-permute-start(f32[12,1,32,4]{2,3,1,0:T(4,128)} %get-tuple-element.47), channel_id=1, source_target_pairs={{0,8},{8,16},{16,24},{1,9},{9,17},{17,25},{2,10},{10,18},{18,26},{... | collective-permute-start | bytes 18440 | tf_op jit(solution)/shard_map/ppermute | solution.py:19
  54.7 9.0 %copy-start.7 = (f32[1024]{0:T(1024)S(1)}, f32[1024]{0:T(1024)}, u32[]{:S(2)}) copy-start(f32[1024]{0:T(1024)} %param.20) | copy-start | bytes 12292
  54.7 9.9 %copy-start.6 = (f32[2048]{0:T(1024)S(1)}, f32[2048]{0:T(1024)}, u32[]{:S(2)}) copy-start(f32[2048]{0:T(1024)} %param.22) | copy-start | bytes 24580
  64.6 11.3 %copy-start.10 = (f32[768]{0:T(1024)S(1)}, f32[768]{0:T(1024)}, u32[]{:S(2)}) copy-start(f32[768]{0:T(1024)} %param.24) | copy-start | bytes 9220
  68.9 10.3 %copy-start.2 = (f32[192,768]{1,0:T(8,128)S(1)}, f32[192,768]{1,0:T(8,128)}, u32[]{:S(2)}) copy-start(f32[192,768]{1,0:T(8,128)} %bitcast_multiply_fusion.1) | copy-start | bytes 1769476
  79.3 0.8 copy-start.4
  87.5 4.8 %collective-permute-start.2 = (bf16[12,1,32,4]{0,2,3,1:T(8,128)(2,1)S(1)}, bf16[12,1,32,4]{0,2,3,1:T(8,128)(2,1)S(1)}, u32[]{:S(2)}, u32[]{:S(2)}) collective-permute-start(bf16[12,1,32,4]{0,2,3,1:T(8,128)(2,1)S(1)} %get-tuple-element.48), channel_id=1, source_target_pairs={{0,8},{8,16},{16,24},{1,9},{9,17},{17,25},{2,10},{10,18},{18,26},{... | collective-permute-start | bytes 9224 | tf_op jit(solution)/shard_map/ppermute | solution.py:19
  89.7 3.1 %collective-permute-start.3 = (bf16[12,1,32,4]{0,2,3,1:T(8,128)(2,1)S(1)}, bf16[12,1,32,4]{0,2,3,1:T(8,128)(2,1)S(1)}, u32[]{:S(2)}, u32[]{:S(2)}) collective-permute-start(bf16[12,1,32,4]{0,2,3,1:T(8,128)(2,1)S(1)} %get-tuple-element.49), channel_id=1, source_target_pairs={{8,0},{16,8},{24,16},{9,1},{17,9},{25,17},{10,2},{18,10},{26,18},{... | collective-permute-start | bytes 9224 | tf_op jit(solution)/shard_map/ppermute | solution.py:22
  115.2 104.9 %all-reduce.11.cloned.1.call-start = ((), (), s32[]{:S(2)}) async-start(), calls=%async_computation.3 | async-start | bytes 278528 | tf_op jit(solution)/shard_map/psum | solution.py:155
Sparse Core Ops, SparseCore 0:
  9.6 36.0 all-gather.2
  47.2 28.5 all-gather.4
  115.3 72.2 all-reduce.8
  189.9 30.1 all-reduce.10
